TPU v7x, 256 devices: a whole 4x4x8 slice. The times are simulated.
256 devices in a mesh: seq: 128 (over y_hi, x, z, core), dp: 2 (over y_lo).
Axes of the slice: x: 4, y: 4 (y_hi: 2, y_lo: 2; y = y_hi * 2 + y_lo), z: 8, core: 2. Of those that a mesh axis runs over, the one named last changes fastest.
Arguments:
- spectrum: bfloat16 [128, 64, 2, 1025], P('seq', 'dp'), parts along dimension 1, may hold values from -6 to 6
- band_table: int32 [60, 2], replicated, may hold values from 0 to 1024, as said below
- band_weight: bfloat16 [60, 2, 64, 384], replicated, may hold values from -0.5 to 0.5
- qkv_weight: bfloat16 [2, 384, 1152], replicated, may hold values from -1.5 to 1.5
- out_weight: bfloat16 [2, 384, 384], replicated, may hold values from -0.3125 to 0.3125
- ff_in_weight: bfloat16 [2, 384, 768], replicated, may hold values from -0.3125 to 0.3125
- ff_out_weight: bfloat16 [2, 768, 384], replicated, may hold values from -0.21875 to 0.21875
- norm_gains: float32 [6, 384], replicated, may hold values from 0.1 to 1.9
Outputs:
- hidden_out: bfloat16 [128, 64, 60, 384], P('seq', 'dp'), parts along dimension 1
There are 2 independent parts, one for each index of `dp`. A program takes and returns all parts, laid end to end along the dimension named above; an argument that names none is the same for every part. Nothing has to cross between parts.
Inputs may be any that keep to these rules, and one draw needn't show every extreme that they name: `band_table`: row n holds band n's first bin and its number of bins; each band lies inside the 1025 bins and has 2 to 64 bins, the last band exactly 64; bands intersect at low frequencies.
All inputs are finite; a program needn't handle non-finite values.
Results may differ from a plain program's by a relative error of at most 0.017.
Values may be sent and summed in bfloat16 or wider, within the bound.
A program may use at most 128 MiB of HBM per device.

v0:
```python
import math

import jax
import jax.numpy as jnp
from jax import lax
from jax.sharding import PartitionSpec as P

HEADS = 8
SPAN = 64


EPSILON = 0.05


def normalize(values, gain_row):
    return (
        values * lax.rsqrt(jnp.mean(values * values, axis=-1, keepdims=True) + EPSILON) * gain_row
    )


def rotate(tensor, positions):
    half_size = tensor.shape[-1] // 2
    frequency = 10000.0 ** (-jnp.arange(half_size, dtype=jnp.float32) / half_size)
    angles = positions[..., None] * frequency
    cosine = jnp.cos(angles)
    sine_part = jnp.sin(angles)
    first_half = tensor[..., :half_size]
    second_half = tensor[..., half_size:]
    return jnp.concatenate(
        [
            first_half * cosine - second_half * sine_part,
            second_half * cosine + first_half * sine_part,
        ],
        axis=-1,
    )


def project(stream, weights, gain_row, positions):
    normed = normalize(stream.astype(jnp.float32), gain_row).astype(jnp.bfloat16)
    mixture = jnp.dot(normed, weights, preferred_element_type=jnp.float32)
    model_width = stream.shape[-1]
    head_shape = stream.shape[:-1] + (HEADS, model_width // HEADS)
    queries = (
        rotate(mixture[..., :model_width].reshape(head_shape), positions)
        .astype(jnp.bfloat16)
        .reshape(stream.shape)
    )
    key_rows = (
        rotate(mixture[..., model_width : 2 * model_width].reshape(head_shape), positions)
        .astype(jnp.bfloat16)
        .reshape(stream.shape)
    )
    value_rows = mixture[..., 2 * model_width :].astype(jnp.bfloat16)
    return (queries, key_rows, value_rows)


def attend_rows(queries, key_rows, value_rows):
    row_count, length, model_width = queries.shape
    head_size = model_width // HEADS
    head_shape = (row_count, length, HEADS, head_size)
    scores = jnp.einsum(
        "rshd,rthd->rhst",
        queries.reshape(head_shape),
        key_rows.reshape(head_shape),
        preferred_element_type=jnp.float32,
    ) / math.sqrt(head_size)
    weights = jax.nn.softmax(scores, axis=-1).astype(jnp.bfloat16)
    context = jnp.einsum(
        "rhst,rthd->rshd",
        weights,
        value_rows.reshape(head_shape),
        preferred_element_type=jnp.float32,
    )
    return context.astype(jnp.bfloat16).reshape(row_count, length, model_width)


def attend_time(queries, key_rows, value_rows):
    context = attend_rows(
        jnp.swapaxes(queries, 0, 1), jnp.swapaxes(key_rows, 0, 1), jnp.swapaxes(value_rows, 0, 1)
    )
    return jnp.swapaxes(context, 0, 1)


def finish(stream, context, weights):
    return (
        stream.astype(jnp.float32) + jnp.dot(context, weights, preferred_element_type=jnp.float32)
    ).astype(jnp.bfloat16)


def feed_forward(stream, weight_in, weight_out, gain_row):
    normed = normalize(stream.astype(jnp.float32), gain_row).astype(jnp.bfloat16)
    active = jax.nn.gelu(
        jnp.dot(normed, weight_in, preferred_element_type=jnp.float32), approximate=True
    ).astype(jnp.bfloat16)
    return (
        stream.astype(jnp.float32) + jnp.dot(active, weight_out, preferred_element_type=jnp.float32)
    ).astype(jnp.bfloat16)


def flatten_items(block):
    return block.reshape(block.shape[0], block.shape[2], block.shape[3])


def body(
    spectrum,
    band_table,
    band_weight,
    qkv_weight,
    out_weight,
    ff_in_weight,
    ff_out_weight,
    norm_gains,
):
    frame_count, batch_size, channel_count, bin_count = spectrum.shape
    band_count = band_table.shape[0]
    offsets = jnp.arange(SPAN, dtype=jnp.int32)
    targets = (band_table[:, 0:1] + offsets[None, :]).reshape(-1)
    valid = (offsets[None, :] < band_table[:, 1:2]).reshape(-1)
    chosen = (
        (jnp.arange(bin_count, dtype=jnp.int32)[:, None] == targets[None, :]) & valid[None, :]
    ).astype(jnp.bfloat16)
    features = jnp.einsum(
        "fbcq,qm->fbcm", spectrum, chosen, preferred_element_type=jnp.float32
    ).astype(jnp.bfloat16)
    features = features.reshape(frame_count, batch_size, channel_count, band_count, SPAN)
    embedded = jnp.einsum(
        "fbcnj,ncjd->fbnd", features, band_weight, preferred_element_type=jnp.float32
    )
    model_width = embedded.shape[-1]
    stream = normalize(embedded, norm_gains[0]).astype(jnp.bfloat16)
    stream = stream.reshape(frame_count * batch_size, band_count, model_width)
    band_positions = jnp.arange(band_count, dtype=jnp.float32).reshape(1, band_count, 1)
    triple = project(stream, qkv_weight[0], norm_gains[1], band_positions)
    stream = finish(stream, attend_rows(triple[0], triple[1], triple[2]), out_weight[0])
    stream = feed_forward(stream, ff_in_weight[0], ff_out_weight[0], norm_gains[2])
    groups = lax.axis_size("seq")
    pair_count = batch_size * band_count
    per_group = pair_count // groups
    stream = stream.reshape(frame_count, groups, per_group, model_width)
    block = lax.all_to_all(stream, "seq", split_axis=1, concat_axis=0, tiled=True)
    flat = flatten_items(block)
    length = flat.shape[0]
    frame_positions = jnp.arange(length, dtype=jnp.float32).reshape(length, 1, 1)
    parts = project(flat, qkv_weight[1], norm_gains[3], frame_positions)
    mixed_block = finish(flat, attend_time(parts[0], parts[1], parts[2]), out_weight[1])
    result_block = feed_forward(mixed_block, ff_in_weight[1], ff_out_weight[1], norm_gains[4])
    regrouped = result_block.reshape(block.shape)
    stream = lax.all_to_all(regrouped, "seq", split_axis=0, concat_axis=1, tiled=True)
    stream = stream.reshape(frame_count, pair_count, model_width)
    result = normalize(stream.astype(jnp.float32), norm_gains[5]).astype(jnp.bfloat16)
    return result.reshape(frame_count, batch_size, band_count, model_width)


def solution(mesh):
    in_specs = (P("seq", "dp", None, None), P(), P(), P(), P(), P(), P(), P())
    out_specs = P("seq", "dp", None, None)
    return jax.shard_map(body, mesh=mesh, in_specs=in_specs, out_specs=out_specs, check_vma=False)
```

profile of v0, /device:TPU:7, one launch (start us, length us, event | category | flops | bytes accessed | tf_op | source)
XLA Modules:
  0.0 240.3 jit_solution(5047683648009683275)
XLA Ops:
  0.0 1.0 slice_reduce_fusion
  1.0 0.8 slice_bitcast_fusion
  2.1 3.8 %fusion.33 = bf16[32,2,3840]{2,0,1:T(8,128)(2,1)S(1)} fusion(s32[3840]{0:T(1024)S(1)} %add.123, pred[3840]{0:T(1024)(128)(4,1)S(1)} %lt.23, bf16[32,2,1025]{2,1,0:T(2,128)(2,1)S(1)} %bitcast.135), kind=kOutput, calls=%fused_computation.35 | convolution fusion | flops 511925760 | bytes 641920 | tf_op jit(solution)/shard_map/fbcq,qm->fbcm/dot_general | solution.py:122
  5.9 1.1 reshape.338
  6.9 4.3 %fusion.67 = (f32[32,60]{0,1:T(8,128)S(1)}, f32[60,32,384,1]{2,1,3,0:T(8,128)S(1)}) fusion(bf16[60,2,64,384]{3,2,1,0:T(8,128)(2,1)} %param.10, bf16[32,2,60,64]{3,2,0,1:T(8,128)(2,1)S(1)} %reshape.338), kind=kOutput, calls=%fused_computation.86 | convolution fusion | flops 190216320 | bytes 9346560 | tf_op jit(solution)/shard_map/fbcnj,ncjd->fbnd/dot_general | solution.py:126
  11.3 0.7 fusion.51
  12.0 0.4 fusion.93
  12.4 0.3 copy-done.5
  12.7 2.8 %fusion.81 = f32[32,60,1152]{2,1,0:T(8,128)S(1)} fusion(bf16[32,60,384]{2,0,1:T(8,128)(2,1)S(1)} %fusion.93, bf16[2,384,1152]{2,1,0:T(8,128)(2,1)S(1)} %copy-done.5), kind=kOutput, calls=%fused_computation.99 | convolution fusion | flops 1698693120 | bytes 11206656 | tf_op jit(solution)/shard_map/dot_general | solution.py:40
  15.6 1.4 slice.200
  17.0 2.5 %fusion.146 = (f32[32,60,384]{2,1,0:T(8,128)}, f32[32,60,384]{2,1,0:T(8,128)S(1)}) fusion(f32[32,60,1152]{2,1,0:T(8,128)S(1)} %fusion.81), kind=kLoop, calls=%fused_computation.173 | loop fusion | bytes 11796480 | tf_op jit(solution)/shard_map/slice | solution.py:49
  19.5 4.5 %copy.121 = bf16[32,60,384]{1,2,0:T(8,128)(2,1)} copy(bf16[32,60,384]{2,1,0:T(8,128)(2,1)} %slice.200) | data formatting | bytes 2949120 | tf_op jit(solution)/shard_map/reshape | solution.py:71
  23.9 5.9 %copy.127 = f32[32,60,384]{1,2,0:T(8,128)} copy(f32[32,60,384]{2,1,0:T(8,128)} %get-tuple-element.13) | data formatting | bytes 5898240 | tf_op jit(solution)/shard_map/reshape | solution.py:49
  30.0 4.2 %copy.124 = f32[32,60,384]{1,2,0:T(8,128)} copy(f32[32,60,384]{2,1,0:T(8,128)S(1)} %get-tuple-element.14) | data formatting | bytes 5898240 | tf_op jit(solution)/shard_map/reshape | solution.py:44
  34.2 5.6 %subtract_convert_fusion = (bf16[32,60,8,24]{1,3,2,0:T(8,128)(2,1)S(1)}, bf16[32,60,8,24]{1,3,2,0:T(8,128)(2,1)S(1)}, bf16[32,60,8,24]{1,3,2,0:T(8,128)(2,1)S(1)}, bf16[32,60,8,24]{1,3,2,0:T(8,128)(2,1)S(1)}) fusion(f32[32,60,8,48]{1,3,2,0:T(8,128)} %bitcast.136, f32[60,24]{0,1:T(8,128)S(1)} %get-tuple-element.34, f32[60,24]{0,1:T(8,128)S(1)} %get-tuple-element.33, ...), kind=kLoop, calls=%fused_computation.64 | loop fusion | flops 5898240 | bytes 8858880 | tf_op jit(solution)/shard_map/convert.8
  39.8 1.8 fusion.44
  41.7 12.2 %fusion.148 = (f32[32,8,60]{2,1,0:T(8,128)S(1)}, f32[32,8,60,60]{2,3,1,0:T(8,128)S(1)}) fusion(f32[32,8,60,60]{2,3,1,0:T(8,128)S(1)} %fusion.44), kind=kOutput, calls=%fused_computation.175 | output fusion | flops 3686459 | bytes 7434240 | tf_op jit(solution)/shard_map/sub | solution.py:67
  53.8 3.5 %fusion.78 = bf16[32,8,48,60]{3,2,1,0:T(8,128)(2,1)} fusion(bf16[32,60,8,48]{1,3,2,0:T(8,128)(2,1)S(1)} %bitcast.140, f32[32,8,60,60]{2,3,1,0:T(8,128)S(1)} %get-tuple-element.38, f32[32,8,60]{2,1,0:T(8,128)S(1)} %get-tuple-element.37), kind=kOutput, calls=%fused_computation.96 | convolution fusion | flops 91054080 | bytes 6696960 | tf_op jit(solution)/shard_map/rhst,rthd->rshd/dot_general | solution.py:68
  57.3 4.3 %copy.113 = bf16[32,60,384]{2,0,1:T(8,128)(2,1)S(1)} copy(bf16[32,60,384]{1,2,0:T(8,128)(2,1)} %bitcast.141) | data formatting | bytes 2949120 | tf_op jit(solution)/shard_map/reshape | solution.py:74
  61.6 2.2 fusion.59
  63.9 0.4 fusion.61
  64.3 0.8 copy-done.8
  65.1 3.1 %fusion.17 = bf16[32,60,768]{2,1,0:T(8,128)(2,1)S(1)} fusion(bf16[32,60,384]{2,0,1:T(8,128)(2,1)S(1)} %fusion.61, bf16[2,384,768]{2,1,0:T(8,128)(2,1)S(1)} %copy-done.8), kind=kOutput, calls=%fused_computation.25 | convolution fusion | flops 1145733120 | bytes 5013504 | tf_op jit(solution)/shard_map/dot_general | solution.py:93
  68.2 3.1 %fusion.62 = bf16[32,60,384]{2,0,1:T(8,128)(2,1)S(1)} fusion(bf16[32,60,384]{2,0,1:T(8,128)(2,1)S(1)} %get-tuple-element.40, bf16[32,60,768]{2,1,0:T(8,128)(2,1)S(1)} %fusion.17, bf16[2,768,384]{2,1,0:T(8,128)(2,1)S(1)} %copy-done.9), kind=kOutput, calls=%fused_computation.78 | convolution fusion | flops 1134673920 | bytes 6684672 | tf_op jit(solution)/shard_map/dot_general | solution.py:96
  71.4 0.5 copy.98
  71.9 11.2 %reshape.343 = bf16[1,128,15,384]{3,2,1,0:T(8,128)(2,1)} reshape(bf16[32,60,384]{2,1,0:T(8,128)(2,1)S(1)} %copy.98) | data formatting | bytes 2949120 | tf_op jit(solution)/shard_map/reshape | solution.py:139
  83.1 16.0 %all-to-all-start = ((bf16[1,128,15,384]{3,2,0,1:T(8,128)(2,1)}), bf16[1,128,15,384]{3,2,0,1:T(8,128)(2,1)S(1)}, u32[]{:S(2)}, u32[]{:S(2)}) async-start(bf16[1,128,15,384]{3,2,0,1:T(8,128)(2,1)} %bitcast.25), calls=%async_computation | async-start | bytes 3145728 | tf_op jit(solution)/shard_map/all_to_all | solution.py:140
  99.1 0.1 fusion.134
  99.2 40.6 %all-to-all-done = bf16[1,128,15,384]{3,2,0,1:T(8,128)(2,1)S(1)} async-done(((bf16[1,128,15,384]{3,2,0,1:T(8,128)(2,1)}), bf16[1,128,15,384]{3,2,0,1:T(8,128)(2,1)S(1)}, u32[]{:S(2)}, u32[]{:S(2)}) %all-to-all-start) | async-done | bytes 1474592 | tf_op jit(solution)/shard_map/all_to_all | solution.py:140
  139.9 0.4 fusion.55
  140.3 2.7 %fusion.91 = f32[128,15,1152]{2,0,1:T(8,128)S(1)} fusion(f32[384]{0:T(512)S(1)} %get-tuple-element.6, f32[128,15]{0,1:T(8,128)S(1)} %add_rsqrt_fusion.5, bf16[1,128,15,384]{3,2,0,1:T(8,128)(2,1)S(1)} %all-to-all-done, bf16[2,384,1152]{2,1,0:T(8,128)(2,1)S(1)} %copy-done.6), kind=kOutput, calls=%fused_computation.103 | convolution fusion | flops 1701642240 | bytes 11315200 | tf_op jit(solution)/shard_map/dot_general | solution.py:40
  143.0 0.2 fusion.87
  143.2 3.3 %fusion.147 = (f32[128,15,384]{2,0,1:T(8,128)}, f32[128,15,384]{2,0,1:T(8,128)}) fusion(f32[128,15,1152]{2,0,1:T(8,128)S(1)} %fusion.91), kind=kLoop, calls=%fused_computation.174 | loop fusion | bytes 11796480 | tf_op jit(solution)/shard_map/slice | solution.py:49
  146.5 2.1 copy.101
  148.6 3.5 %copy.103 = f32[128,15,384]{0,2,1:T(8,128)} copy(f32[128,15,384]{2,0,1:T(8,128)} %get-tuple-element.15) | data formatting | bytes 5898240 | tf_op jit(solution)/shard_map/slice | solution.py:49
  152.1 3.5 %copy.102 = f32[128,15,384]{0,2,1:T(8,128)} copy(f32[128,15,384]{2,0,1:T(8,128)} %get-tuple-element.16) | data formatting | bytes 5898240 | tf_op jit(solution)/shard_map/slice | solution.py:44
  155.6 3.6 %subtract_convert_fusion.2 = (bf16[128,15,8,24]{0,3,2,1:T(8,128)(2,1)S(1)}, bf16[128,15,8,24]{0,3,2,1:T(8,128)(2,1)S(1)}, bf16[128,15,8,24]{0,3,2,1:T(8,128)(2,1)S(1)}, bf16[128,15,8,24]{0,3,2,1:T(8,128)(2,1)S(1)}) fusion(f32[128,15,8,48]{0,3,2,1:T(8,128)} %bitcast.138, f32[128,24]{0,1:T(8,128)S(1)} %get-tuple-element.32, ...), kind=kLoop, calls=%fused_computation.116 | loop fusion | flops 5898240 | bytes 8871936 | tf_op jit(solution)/shard_map/convert.3
  159.2 1.2 fusion.94
  160.5 7.4 %fusion.149 = (f32[15,8,128]{2,1,0:T(8,128)S(1)}, f32[15,8,128,128]{2,3,1,0:T(8,128)S(1)}) fusion(f32[15,8,128,128]{2,3,1,0:T(8,128)S(1)} %fusion.94), kind=kOutput, calls=%fused_computation.176 | output fusion | flops 7864447 | bytes 15790080 | tf_op jit(solution)/shard_map/sub | solution.py:67
  167.9 2.3 fusion.79
  170.2 2.4 copy.105
  172.5 3.4 %fusion.63 = (f32[128,15]{0,1:T(8,128)S(1)}, bf16[128,15,384]{2,0,1:T(8,128)(2,1)}) fusion(bf16[2,384,384]{2,1,0:T(8,128)(2,1)} %param.12, bf16[15,128,384]{2,1,0:T(8,128)(2,1)S(1)} %copy.105, bf16[1,128,15,384]{3,2,0,1:T(8,128)(2,1)S(1)} %all-to-all-done), kind=kOutput, calls=%fused_computation.79 | convolution fusion | flops 570652800 | bytes 4726272 | tf_op jit(solution)/shard_map/dot_general | solution.py:86
  175.9 5.9 %fusion.106 = bf16[128,1,15,384]{3,0,2,1:T(8,128)(2,1)S(1)} fusion(bf16[128,15,384]{2,0,1:T(8,128)(2,1)} %get-tuple-element.44, f32[384]{0:T(512)S(1)} %get-tuple-element.10, f32[128,15]{0,1:T(8,128)S(1)} %add_rsqrt_fusion.4, bf16[2,768,384]{2,1,0:T(8,128)(2,1)} %param.14, bf16[2,384,768]{2,1,0:T(8,128)(2,1)} %param.13), kind=kOutput, calls=%fused_computation.121 | convolution fusion | flops 2283356160 | bytes 5612544 | tf_op jit(solution)/shard_map/dot_general | solution.py:96
  181.8 0.9 copy.106
  182.7 49.0 %all_to_all.8 = bf16[128,1,15,384]{3,2,1,0:T(8,128)(2,1)S(1)} all-to-all(bf16[128,1,15,384]{3,2,1,0:T(8,128)(2,1)S(1)} %copy.106), channel_id=1, replica_groups=mesh['seq'=128,'dp'=2] {'seq'}, dimensions={0} | all-to-all | bytes 2949120 | tf_op jit(solution)/shard_map/all_to_all | solution.py:148
  231.7 0.4 multiply_reduce_fusion.2
  232.5 4.2 %reshape.353 = f32[1,32,60,384]{3,0,2,1:T(1,128)} reshape(bf16[128,1,15,384]{3,2,1,0:T(8,128)(2,1)S(1)} %all_to_all.8) | data formatting | bytes 4423680 | tf_op jit(solution)/shard_map/convert_element_type | solution.py:150
  236.8 3.3 %fusion.73 = bf16[1,32,60,384]{3,1,2,0:T(8,128)(2,1)} fusion(f32[1,32,60,384]{3,0,2,1:T(1,128)} %reshape.353, f32[384]{0:T(512)S(1)} %get-tuple-element.5, f32[32,60]{0,1:T(8,128)S(1)} %copy.109), kind=kLoop, calls=%fused_computation.93 | loop fusion | flops 2211840 | bytes 4432896 | tf_op jit(solution)/shard_map/convert_element_type | solution.py:150
  (34 shorter events, 0.9 us)
Async XLA Ops:
  0.0 2.0 copy-start
  11.2 1.5 copy-start.5
  11.9 3.6 %copy-start.2 = (bf16[1,32,60,384]{3,1,2,0:T(8,128)(2,1)}, bf16[1,32,60,384]{3,1,2,0:T(8,128)(2,1)S(1)}, u32[]{:S(2)}) copy-start(bf16[1,32,60,384]{3,1,2,0:T(8,128)(2,1)S(1)} %get-tuple-element.12) | copy-start | bytes 4423684
  41.6 12.2 %copy-start.4 = (bf16[32,60,384]{1,2,0:T(8,128)(2,1)S(1)}, bf16[32,60,384]{1,2,0:T(8,128)(2,1)}, u32[]{:S(2)}) copy-start(bf16[32,60,384]{1,2,0:T(8,128)(2,1)} %copy.121) | copy-start | bytes 4423684
  57.3 4.3 %copy-start.3 = (bf16[1,32,60,384]{3,1,2,0:T(8,128)(2,1)S(1)}, bf16[1,32,60,384]{3,1,2,0:T(8,128)(2,1)}, u32[]{:S(2)}) copy-start(bf16[1,32,60,384]{3,1,2,0:T(8,128)(2,1)} %copy-done.2) | copy-start | bytes 4423684
  63.8 1.3 copy-start.8
  65.1 3.1 %copy-start.9 = (bf16[2,768,384]{2,1,0:T(8,128)(2,1)S(1)}, bf16[2,768,384]{2,1,0:T(8,128)(2,1)}, u32[]{:S(2)}) copy-start(bf16[2,768,384]{2,1,0:T(8,128)(2,1)} %param.14) | copy-start | bytes 3538948
  83.1 57.2 %copy-start.6 = (bf16[2,384,1152]{2,1,0:T(8,128)(2,1)S(1)}, bf16[2,384,1152]{2,1,0:T(8,128)(2,1)}, u32[]{:S(2)}) copy-start(bf16[2,384,1152]{2,1,0:T(8,128)(2,1)} %param.11) | copy-start | bytes 5308420
  83.1 56.8 %all-to-all-start = ((bf16[1,128,15,384]{3,2,0,1:T(8,128)(2,1)}), bf16[1,128,15,384]{3,2,0,1:T(8,128)(2,1)S(1)}, u32[]{:S(2)}, u32[]{:S(2)}) async-start(bf16[1,128,15,384]{3,2,0,1:T(8,128)(2,1)} %bitcast.25), calls=%async_computation | async-start | bytes 3145728 | tf_op jit(solution)/shard_map/all_to_all | solution.py:140
  160.5 7.4 %copy-start.7 = (bf16[15,128,384]{1,2,0:T(8,128)(2,1)S(1)}, bf16[15,128,384]{1,2,0:T(8,128)(2,1)}, u32[]{:S(2)}) copy-start(bf16[15,128,384]{1,2,0:T(8,128)(2,1)} %copy.101) | copy-start | bytes 4423684
  232.5 7.5 %copy-start.1 = (bf16[1,32,2,1025]{3,2,1,0:T(2,128)(2,1)S(1)}, bf16[1,32,2,1025]{3,2,1,0:T(2,128)(2,1)}, u32[]{:S(2)}) copy-start(bf16[1,32,2,1025]{3,2,1,0:T(2,128)(2,1)} %param.8) | copy-start | bytes 393604
where the time goes:
time: 245 us; the launch traced here: 240 us
  local copies, waits for them, and re-layouts  59 us (24%)
  blocking collectives  49 us (20%)
  waiting for transfers between devices  40.6 us (17%)
  matrix products  40.2 us (16%)
  other arithmetic  34.8 us (14%)
  starting transfers between devices  16 us (7%)
    all_to_all x1, blocking collectives, body(): lax.all_to_all(regrouped, 'seq', split_axis=0, concat_axis=1, tiled=True)  49 us
    all_to_all x1, waiting for transfers between devices, body(): lax.all_to_all(stream, 'seq', split_axis=1, concat_axis=0, tiled=True)  40.6 us
    sub x2, other arithmetic, attend_rows(): weights = jax.nn.softmax(scores, axis=-1).astype(jnp.bfloat16)  19.5 us
    all_to_all x1, starting transfers between devices, body(): lax.all_to_all(stream, 'seq', split_axis=1, concat_axis=0, tiled=True)  16 us
    reshape x1, local copies, waits for them, and re-layouts, body(): stream = stream.reshape(frame_count, groups, per_group, model_width)  11.2 us
    slice x3, local copies, waits for them, and re-layouts, project(): mixture[..., model_width:2 * model_width].reshape(head_shape)  9.24 us
    another operation x2, other arithmetic  9.22 us
    dot_general x2, matrix products, feed_forward(): jnp.dot(active, weight_out, preferred_element_type=jnp.float32)  8.97 us
  transfers between devices with their start and end apart: 1, of which 1 were waited for; matrix products, arithmetic and copies ran while one was open for 0% of the time, Pallas kernels for 0%

commit v1 on v0

v1 whole, which is shorter than its diff:
```python
import functools
import math

import jax
import jax.numpy as jnp
import numpy as np
from jax import lax
from jax.experimental import pallas as pl
from jax.experimental.pallas import tpu as pltpu
from jax.sharding import PartitionSpec as P

D = 384
HEADS = 8
HEAD = 48
HALF = 24
SPAN = 64
EPSILON = 0.05
WIDE = 512
CHUNK = 8
SLOTS = 64
TILE = 256
NEG = -1e30
MESH = pl.DeviceIdType.MESH


def head_columns():
    rotary = np.zeros((D, WIDE), np.float32)
    value = np.zeros((D, WIDE), np.float32)
    for head in range(HEADS):
        base = (head // 2) * 128
        for i in range(HEAD):
            half, j = divmod(i, HALF)
            rotary[head * HEAD + i, base + 64 * half + (head % 2) * HALF + j] = 1
            value[head * HEAD + i, base + 64 * (head % 2) + i] = 1
    return rotary, value


def rotary_tables(positions):
    frequency = 10000.0 ** (-np.arange(HALF, dtype=np.float64) / HALF)
    angles = positions[:, None].astype(np.float64) * frequency
    cosine = np.zeros((len(positions), 128))
    sine = np.zeros((len(positions), 128))
    for head in range(2):
        for half in range(2):
            at = 64 * half + head * HALF
            cosine[:, at : at + HALF] = np.cos(angles)
            sine[:, at : at + HALF] = np.sin(angles) * (1 if half else -1)
    scale = math.log2(math.e) / math.sqrt(HEAD)
    return [cosine * scale, sine * scale, cosine, sine]


def swap_matrix(outer, inner):
    result = np.zeros((outer * inner, outer * inner), np.float32)
    for i in range(outer):
        for j in range(inner):
            result[j * outer + i, i * inner + j] = 1
    return result


def normalize(values, gain):
    return (
        values
        * lax.rsqrt(jnp.mean(values * values, axis=-1, keepdims=True) + EPSILON)
        * gain
    )


def dot(a, b):
    return jnp.dot(a, b, preferred_element_type=jnp.float32)


def kernel(
    groups,
    bands,
    table,
    spectrum,
    gains,
    band_hbm,
    qkv_hbm,
    mix_hbm,
    ff_in_hbm,
    ff_out_hbm,
    rope_hbm,
    rotary_hbm,
    value_hbm,
    spread_hbm,
    swap_hbm,
    out_ref,
    band_w,
    qkv_raw,
    mix_raw,
    ff_in,
    ff_out,
    rope,
    rotary_p,
    value_p,
    spread_p,
    swap_p,
    qkv_w,
    mix_w,
    embedded,
    stream,
    arrived,
    turned,
    hidden,
    leaving,
    q_s,
    k_s,
    v_s,
    c_s,
    lanes,
    load_sem,
    send_sem,
    recv_sem,
):
    me = lax.axis_index("seq")
    half_rows = groups * CHUNK
    quarter = bands // 4

    loads = [
        pltpu.make_async_copy(src, dst, load_sem.at[i])
        for i, (src, dst) in enumerate(
            [
                (rotary_hbm, rotary_p),
                (value_hbm, value_p),
                (qkv_hbm, qkv_raw),
                (spread_hbm, spread_p),
                (mix_hbm, mix_raw),
            ]
            + [
                (
                    band_hbm.at[pl.ds(i * quarter, quarter)],
                    band_w.at[pl.ds(i * quarter, quarter)],
                )
                for i in range(4)
            ]
            + [
                (swap_hbm, swap_p),
                (rope_hbm, rope),
                (ff_in_hbm, ff_in),
                (ff_out_hbm, ff_out),
            ]
        )
    ]
    for load in loads:
        load.start()

    barrier = pltpu.get_barrier_semaphore()

    def greet(step, carry):
        pl.semaphore_signal(
            barrier,
            inc=1,
            device_id={"seq": lax.rem(me + step, groups)},
            device_id_type=MESH,
        )
        return carry

    lax.fori_loop(1, groups, greet, 0)

    lane = lax.broadcasted_iota(jnp.int32, (1, 128), 1)
    low = lane < 64
    inner = jnp.where(low, lane, lane - 64)
    even = inner < HALF

    row = lax.broadcasted_iota(jnp.int32, (TILE, 128), 0)
    column = lax.broadcasted_iota(jnp.int32, (TILE, 128), 1)
    ones = jnp.where((row < 128) == (column < 64), 1.0, 0.0).astype(jnp.bfloat16)
    for i in range(8):
        v_s[i, :, pl.ds(128, 128)] = ones
    embedded[pl.ds(bands * 32, (SLOTS - bands) * 32), :] = jnp.zeros(
        ((SLOTS - bands) * 32, D), jnp.bfloat16
    )

    def prepare(layer):
        for part in range(3):
            source = qkv_raw[layer, :, pl.ds(part * D, D)]
            spread = value_p[...] if part == 2 else rotary_p[...]
            qkv_w[layer, :, pl.ds(part * WIDE, WIDE)] = dot(source, spread).astype(
                jnp.bfloat16
            )
        mix_w[layer] = dot(spread_p[...], mix_raw[layer]).astype(jnp.bfloat16)

    for load in loads[:5]:
        load.wait()
    prepare(0)

    gain = gains[0:1, :]
    for i in range(lanes.shape[0]):
        lanes[i] = spectrum[:, pl.ds(128 * i, 128)]

    def embed(step, carry):
        for k in range(5):
            band = step * 5 + k
            start = table[band, 0]
            width = table[band, 1]
            block = lax.div(start, 128)
            offset = lax.rem(start, 128)
            window = jnp.concatenate([lanes[block], lanes[block + 1]], axis=1)
            first = pltpu.roll(window[0:32], lax.rem(256 - offset, 256), 1)[:, :128]
            second = pltpu.roll(window[32:64], lax.rem(320 - offset, 256), 1)[:, :128]
            picked = jnp.where(low, first, second)
            picked = jnp.where(inner < width, picked, 0.0).astype(jnp.bfloat16)
            rows = normalize(dot(picked, band_w[band]), gain)
            at = pl.multiple_of(band * 32, 32)
            embedded[pl.ds(at, 32), :] = rows.astype(jnp.bfloat16)
        return carry

    for i in range(4):
        loads[5 + i].wait()
        lax.fori_loop(i * 3, i * 3 + 3, embed, 0)
    for load in loads[9:]:
        load.wait()

    def turn_bands(step, carry):
        band_at = lax.rem(step, 4) * 16
        row_at = (step // 4) * 16
        block = jnp.concatenate(
            [
                embedded[pl.ds(pl.multiple_of((band_at + i) * 32 + row_at, 16), 16), :]
                for i in range(16)
            ],
            axis=0,
        )
        result = dot(swap_p[0], block).astype(jnp.bfloat16)
        for i in range(16):
            at = pl.multiple_of((row_at + i) * SLOTS + band_at, 16)
            stream[pl.ds(at, 16), :] = result[16 * i : 16 * i + 16]
        return carry

    lax.fori_loop(0, 8, turn_bands, 0)

    def sublayer(layer, x, mask):
        at = layer * 4
        first_gain = gains[1 + 2 * layer : 2 + 2 * layer, :]
        second_gain = gains[2 + 2 * layer : 3 + 2 * layer, :]
        xf = x.astype(jnp.float32)
        normed = normalize(xf, first_gain).astype(jnp.bfloat16)
        tables = [rope[at + i] for i in range(4)]
        for part in range(2):
            mixed = dot(normed, qkv_w[layer, :, pl.ds(part * WIDE, WIDE)])
            for r in range(2):
                for pair in range(4):
                    value = mixed[128 * r : 128 * r + 128, 128 * pair : 128 * pair + 128]
                    value = (
                        value * tables[2 * part]
                        + pltpu.roll(value, 64, 1) * tables[2 * part + 1]
                    )
                    if part == 0:
                        q_s[pl.ds(128 * r, 128), pl.ds(128 * pair, 128)] = value.astype(
                            jnp.bfloat16
                        )
                    else:
                        k_s[4 * r + pair, pl.ds(0, 128), :] = jnp.where(
                            even, value, 0.0
                        ).astype(jnp.bfloat16)
                        k_s[4 * r + pair, pl.ds(128, 128), :] = jnp.where(
                            even, 0.0, value
                        ).astype(jnp.bfloat16)
        mixed = dot(normed, qkv_w[layer, :, pl.ds(2 * WIDE, WIDE)])
        for r in range(2):
            for pair in range(4):
                value = mixed[128 * r : 128 * r + 128, 128 * pair : 128 * pair + 128]
                v_s[4 * r + pair, pl.ds(0, 128), pl.ds(0, 128)] = jnp.where(
                    low, value, 0.0
                ).astype(jnp.bfloat16)
                v_s[4 * r + pair, pl.ds(128, 128), pl.ds(0, 128)] = jnp.where(
                    low, 0.0, value
                ).astype(jnp.bfloat16)
        for r in range(2):
            for pair in range(4):
                scores = lax.dot_general(
                    q_s[pl.ds(128 * r, 128), pl.ds(128 * pair, 128)],
                    k_s[4 * r + pair],
                    (((1,), (1,)), ((), ())),
                    preferred_element_type=jnp.float32,
                )
                probs = []
                for head in range(2):
                    score = scores[:, 128 * head : 128 * head + 128]
                    if mask is not None:
                        score = jnp.where(mask, score, NEG)
                    score = score - jnp.max(score, axis=-1, keepdims=True)
                    probs.append(jnp.exp2(score).astype(jnp.bfloat16))
                both = dot(jnp.concatenate(probs, axis=1), v_s[4 * r + pair])
                c_s[pl.ds(128 * r, 128), pl.ds(128 * pair, 128)] = (
                    both[:, :128] / both[:, 128:]
                ).astype(jnp.bfloat16)
        x = (xf + dot(c_s[...], mix_w[layer])).astype(jnp.bfloat16)
        xf = x.astype(jnp.float32)
        normed = normalize(xf, second_gain).astype(jnp.bfloat16)
        active = jax.nn.gelu(dot(normed, ff_in[layer]), approximate=True).astype(
            jnp.bfloat16
        )
        return (xf + dot(active, ff_out[layer])).astype(jnp.bfloat16)

    def send(source, target, place, phase, half):
        at = pl.multiple_of(half * half_rows + target * CHUNK, CHUNK)
        to = pl.multiple_of(half * half_rows + me * CHUNK, CHUNK)

        @pl.when(target != me)
        def _():
            pltpu.make_async_remote_copy(
                src_ref=source.at[pl.ds(at, CHUNK)],
                dst_ref=place.at[pl.ds(to, CHUNK)],
                send_sem=send_sem.at[2 * phase + half],
                recv_sem=recv_sem.at[2 * phase + half],
                device_id={"seq": target},
                device_id_type=MESH,
            ).start()

        @pl.when(target == me)
        def _():
            pltpu.make_async_copy(
                source.at[pl.ds(at, CHUNK)],
                place.at[pl.ds(to, CHUNK)],
                recv_sem.at[2 * phase + half],
            ).start()

    query_at = lax.broadcasted_iota(jnp.int32, (128, 128), 0)
    key_at = lax.broadcasted_iota(jnp.int32, (128, 128), 1)
    key_band = jnp.where(key_at < SLOTS, key_at, key_at - SLOTS)
    band_mask = ((query_at < SLOTS) == (key_at < SLOTS)) & (key_band < bands)

    own = me // (groups // 4)

    def band_step(step, carry):
        half = step // 4
        block = half * 4 + lax.rem(step + own, 4)
        at = pl.multiple_of(block * TILE, TILE)
        stream[pl.ds(at, TILE), :] = sublayer(0, stream[pl.ds(at, TILE), :], band_mask)

        @pl.when(step == 0)
        def _():
            pl.semaphore_wait(barrier, groups - 1)

        def post(i, inner_carry):
            target = lax.rem(step + own, 4) * 32 + lax.rem(me + i, 32)
            send(stream, target, arrived, 0, half)
            return inner_carry

        lax.fori_loop(0, 32, post, 0)
        return carry

    lax.fori_loop(0, 8, band_step, 0)
    prepare(1)

    def time_half(half, carry):
        base = pl.multiple_of(half * half_rows, half_rows)
        whole = arrived.at[pl.ds(base, half_rows)]
        pltpu.make_async_copy(whole, whole, recv_sem.at[half]).wait()
        for k in range(4):
            block = arrived[pl.ds(base + k * TILE, TILE), :]
            result = dot(swap_p[1], block).astype(jnp.bfloat16)
            for i in range(8):
                turned[pl.ds(i * 128 + 32 * k, 32), :] = result[32 * i : 32 * i + 32]

        def time_step(step, inner_carry):
            at = pl.multiple_of(step * TILE, TILE)
            x = sublayer(1, turned[pl.ds(at, TILE), :], None)
            hidden[pl.ds(at, TILE), :] = normalize(
                x.astype(jnp.float32), gains[5:6, :]
            ).astype(jnp.bfloat16)
            return inner_carry

        lax.fori_loop(0, 4, time_step, 0)
        for k in range(4):
            block = jnp.concatenate(
                [hidden[pl.ds(i * 128 + 32 * k, 32), :] for i in range(8)], axis=0
            )
            leaving[pl.ds(base + k * TILE, TILE), :] = dot(swap_p[2], block).astype(
                jnp.bfloat16
            )

        def post(i, inner_carry):
            send(leaving, lax.rem(me + i, groups), out_ref, 1, half)
            return inner_carry

        lax.fori_loop(0, groups, post, 0)
        return carry

    lax.fori_loop(0, 2, time_half, 0)
    for half in range(2):
        whole = out_ref.at[pl.ds(half * half_rows, half_rows)]
        pltpu.make_async_copy(whole, whole, recv_sem.at[2 + half]).wait()
    for i in range(4):
        sent = stream.at[pl.ds(0, half_rows - CHUNK)]
        pltpu.make_async_copy(sent, sent, send_sem.at[i]).wait()


def body(
    spectrum,
    band_table,
    band_weight,
    qkv_weight,
    out_weight,
    ff_in_weight,
    ff_out_weight,
    norm_gains,
):
    _, batch, channels, bins = spectrum.shape
    bands = band_table.shape[0]
    hidden_size = ff_in_weight.shape[-1]
    groups = lax.axis_size("seq")
    rotary, value = head_columns()
    band_positions = np.arange(128) % SLOTS
    rope = np.stack(rotary_tables(band_positions) + rotary_tables(np.arange(128)))
    swaps = np.stack([swap_matrix(16, 16), swap_matrix(32, 8), swap_matrix(8, 32)])
    rows = batch * SLOTS
    flat = jnp.swapaxes(spectrum[0], 0, 1).reshape(channels * batch, bins)
    flat = jnp.pad(flat.astype(jnp.float32), ((0, 0), (0, 1152 - bins)))
    bf16 = jnp.bfloat16
    hbm = pl.BlockSpec(memory_space=pl.ANY)
    vmem = pl.BlockSpec(memory_space=pltpu.VMEM)
    result = pl.pallas_call(
        functools.partial(kernel, groups, bands),
        out_shape=jax.ShapeDtypeStruct((rows, D), bf16),
        in_specs=[pl.BlockSpec(memory_space=pltpu.SMEM), vmem, vmem] + [hbm] * 10,
        out_specs=vmem,
        scratch_shapes=[
            pltpu.VMEM((bands, channels * SPAN, D), bf16),
            pltpu.VMEM((2, D, 3 * D), bf16),
            pltpu.VMEM((2, D, D), bf16),
            pltpu.VMEM((2, D, hidden_size), bf16),
            pltpu.VMEM((2, hidden_size, D), bf16),
            pltpu.VMEM((8, 128, 128), jnp.float32),
            pltpu.VMEM((D, WIDE), bf16),
            pltpu.VMEM((D, WIDE), bf16),
            pltpu.VMEM((WIDE, D), bf16),
            pltpu.VMEM((3, TILE, TILE), bf16),
            pltpu.VMEM((2, D, 3 * WIDE), bf16),
            pltpu.VMEM((2, WIDE, D), bf16),
            pltpu.VMEM((rows, D), bf16),
            pltpu.VMEM((rows, D), bf16),
            pltpu.VMEM((rows, D), bf16),
            pltpu.VMEM((rows // 2, D), bf16),
            pltpu.VMEM((rows // 2, D), bf16),
            pltpu.VMEM((rows, D), bf16),
            pltpu.VMEM((TILE, WIDE), bf16),
            pltpu.VMEM((8, TILE, 128), bf16),
            pltpu.VMEM((8, TILE, 256), bf16),
            pltpu.VMEM((TILE, WIDE), bf16),
            pltpu.VMEM((9, channels * batch, 128), jnp.float32),
            pltpu.SemaphoreType.DMA((13,)),
            pltpu.SemaphoreType.DMA((4,)),
            pltpu.SemaphoreType.DMA((4,)),
        ],
        compiler_params=pltpu.CompilerParams(
            collective_id=0, has_side_effects=True, vmem_limit_bytes=60 * 1024 * 1024
        ),
    )(
        band_table,
        flat,
        norm_gains,
        band_weight.reshape(bands, channels * SPAN, D),
        qkv_weight,
        out_weight,
        ff_in_weight,
        ff_out_weight,
        jnp.asarray(rope, jnp.float32),
        jnp.asarray(rotary, bf16),
        jnp.asarray(value, bf16),
        jnp.asarray(value.T, bf16),
        jnp.asarray(swaps, bf16),
    )
    return result.reshape(1, batch, SLOTS, D)[:, :, :bands]


def solution(mesh):
    in_specs = (P("seq", "dp", None, None), P(), P(), P(), P(), P(), P(), P())
    out_specs = P("seq", "dp", None, None)
    return jax.shard_map(body, mesh=mesh, in_specs=in_specs, out_specs=out_specs, check_vma=False)
```

time: 245 us -> 100 us (0.41); the launches traced: 240 us -> 100 us
  Pallas kernels: 0 us -> 93.6 us
  local copies, waits for them, and re-layouts: 59 us -> 5.68 us
  blocking collectives: 49 us -> 0 us
  waiting for transfers between devices: 40.6 us -> 0 us
  matrix products: 40.2 us -> 0 us
  other arithmetic: 34.8 us -> 0.73 us
  starting transfers between devices: 16 us -> 0 us
    pallas_call x0 -> x1, Pallas kernels: none -> 93.6 us  [body(): pl.pallas_call(functools.partial(kernel, groups, bands), out_shape=jax.Sh...]
    all_to_all x1 -> x0, blocking collectives: 49 us -> none  [body(): lax.all_to_all(regrouped, 'seq', split_axis=0, concat_axis=1, tiled=True)]
    all_to_all x1 -> x0, waiting for transfers between devices: 40.6 us -> none  [body(): lax.all_to_all(stream, 'seq', split_axis=1, concat_axis=0, tiled=True)]
    dot_general x13 -> x0, matrix products: 40.2 us -> none  [the longest x2 8.97 us: feed_forward(): jnp.dot(active, weight_out, preferred_element_type=jnp.float32)]
    reshape x7 -> x0, local copies, waits for them, and re-layouts: 33.3 us -> none  [the longest x1 11.2 us: body(): stream = stream.reshape(frame_count, groups, per_group, model_width)]
    sub x2 -> x0, other arithmetic: 19.5 us -> none  [attend_rows(): weights = jax.nn.softmax(scores, axis=-1).astype(jnp.bfloat16)]
    all_to_all x1 -> x0, starting transfers between devices: 16 us -> none  [body(): lax.all_to_all(stream, 'seq', split_axis=1, concat_axis=0, tiled=True)]
    slice x6 -> x0, local copies, waits for them, and re-layouts: 15.2 us -> none  [the longest x3 9.24 us: project(): mixture[..., model_width:2 * model_width].reshape(head_shape)]
  transfers between devices with their start and end apart: 1 -> 0, of which waited for: 1 -> 0; matrix products, arithmetic and copies ran while one was open for 0% -> 0% of each run, Pallas kernels for 0% -> 0%
where the time goes in v1:
time: 100 us
  Pallas kernels  93.6 us (94%)
  local copies, waits for them, and re-layouts  5.68 us (6%)
    pallas_call x1, Pallas kernels, body(): pl.pallas_call(functools.partial(kernel, groups, bands), out_shape=jax.Sh...  93.6 us
    unnamed x2, local copies, waits for them, and re-layouts  4.75 us

profile of v1, /device:TPU:7, one launch (start us, length us, event | category | flops | bytes accessed | tf_op | source)
XLA Modules:
  0.0 100.0 jit_solution(14138435093256913325)
XLA Ops:
  0.0 1.4 %copy.15.table = s32[60,2]{1,0:T(8,128)} copy(s32[60,2]{0,1:T(2,128)} %param.14) | data formatting | bytes 960 | tf_op args[1]
  1.4 0.9 copy.14
  2.3 0.7 pad_convert_fusion.spectrum
  3.0 93.6 %shard_map.127 = bf16[2048,384]{1,0:T(8,128)(2,1)} custom-call(s32[60,2]{1,0:T(8,128)} %copy.15.table, f32[64,1152]{1,0:T(8,128)} %pad_convert_fusion.spectrum, f32[6,384]{1,0:T(8,128)} %gains.1, bf16[60,128,384]{2,1,0:T(8,128)(2,1)} %bitcast.8, bf16[2,384,1152]{2,1,0:T(8,128)(2,1)} %qkv_hbm.1, bf16[2,384,384]{2,1,0:T(8,128)(2,1)} %mix_hbm.1, ...), custom_call_target="tpu_custom_call" | custom-call | tf_op jit(solution)/shard_map/pallas_call | solution.py:415
  96.6 3.4 %copy.17 = bf16[1,32,60,384]{3,1,2,0:T(8,128)(2,1)} copy(bf16[1,32,60,384]{3,2,1,0:T(8,128)(2,1)} %bitcast.7) | data formatting | bytes 2949120
